TPU v7x, 128 devices: a whole 4x4x4 slice. The times are simulated.
128 devices in a mesh: row: 8 (over y, core), col: 16 (over x, z).
Axes of the slice: x: 4, y: 4, z: 4, core: 2. Of those that a mesh axis runs over, the one named last changes fastest.
Arguments:
- measured: float32 [512, 128, 128], P(('row', 'col')), may hold values from 0 to 2
- positions: int32 [512, 2], P(('row', 'col')), may hold values from 0 to 1920, as said below
- probe: float32 [2, 128, 128], replicated, may hold values from -6 to 6
- prop_phase: float32 [128, 128], replicated, may hold values from -3.140625 to 3.140625
- object_real: float32 [4, 1024, 2048], P(None, 'row', 'col'), may hold values from 0.5 to 1.5
- object_imag: float32 [4, 1024, 2048], P(None, 'row', 'col'), may hold values from -1.8 to 1.8
Outputs:
- new_real: float32 [4, 1024, 2048], P(None, 'row', 'col')
- new_imag: float32 [4, 1024, 2048], P(None, 'row', 'col')
- new_probe: float32 [2, 128, 128], replicated
Inputs may be any that keep to these rules, and one draw needn't show every extreme that they name: `positions`: frame f belongs to device d = f // 4, with r = d // 16 and c = d % 16. Its row lies from max(r * 128 - 64, 0) to min(r * 128 + 64, 896), both ends included; its column from max(c * 128 - 64, 0) to min(c * 128 + 64, 1920). On every device some frame takes the lower end and some frame the upper end of each of the two ranges.
All inputs are finite; a program needn't handle non-finite values.
Results may differ from a plain program's by a relative error of at most 0.0003.
Values sent between devices are 32-bit elements; how exact they have to be, the bound alone decides.
No kernel may reach another device: no remote copies, remote signals or barrier semaphores. Data moves between devices by JAX's collectives and lax.ppermute only.
A program may use at most 128 MiB of HBM per device.

v0:
```python
import math

import jax
import jax.numpy as jnp
from jax import lax
from jax.sharding import PartitionSpec as P

PASSES = 3


object_rate = 0.5
probe_rate = 0.5
highest = lax.Precision.HIGHEST


def with_halo(cells, sides, width):
    for axis, dim in sides:
        count = lax.axis_size(axis)
        ends = count - 1
        head = lax.slice_in_dim(cells, 0, width, axis=dim)
        tail = lax.slice_in_dim(cells, cells.shape[dim] - width, cells.shape[dim], axis=dim)
        cells = jnp.concatenate(
            [
                lax.ppermute(tail, axis, [(i, (i + 1) % count) for i in range(ends)]),
                cells,
                lax.ppermute(head, axis, [((i + 1) % count, i) for i in range(ends)]),
            ],
            axis=dim,
        )
    return cells


def gathered_total(value, axis):
    return lax.all_gather(value, axis).sum(0)


def shifted(value, axis, by):
    devices = lax.axis_size(axis)
    pairs = [(i, i + by) for i in range(devices) if 0 <= i + by < devices]
    return lax.ppermute(value, axis, pairs)


def tables(pixels):
    counter = jnp.arange(pixels, dtype=jnp.int32)
    phases = counter[:, None] * counter[None, :] % pixels
    angles = phases.astype(jnp.float32) * (2.0 * math.pi / pixels)
    norm_scale = 1.0 / math.sqrt(pixels)
    return (jnp.cos(angles) * norm_scale, jnp.sin(angles) * norm_scale)


def transform(real_part, imag_part, cosine_table, sine_table, direction):
    right_re = jnp.einsum(
        "fjk,kl->fjl", real_part, cosine_table, precision=highest
    ) + direction * jnp.einsum("fjk,kl->fjl", imag_part, sine_table, precision=highest)
    right_im = jnp.einsum(
        "fjk,kl->fjl", imag_part, cosine_table, precision=highest
    ) - direction * jnp.einsum("fjk,kl->fjl", real_part, sine_table, precision=highest)
    out_re = jnp.einsum(
        "lj,fjk->flk", cosine_table, right_re, precision=highest
    ) + direction * jnp.einsum("lj,fjk->flk", sine_table, right_im, precision=highest)
    out_im = jnp.einsum(
        "lj,fjk->flk", cosine_table, right_im, precision=highest
    ) - direction * jnp.einsum("lj,fjk->flk", sine_table, right_re, precision=highest)
    return (out_re, out_im)


def multiply(left_re, left_im, right_re, right_im):
    return (left_re * right_re - left_im * right_im, left_re * right_im + left_im * right_re)


def conj_multiply(left_re, left_im, right_re, right_im):
    return (left_re * right_re + left_im * right_im, left_re * right_im - left_im * right_re)


def propagate(real_part, imag_part, kernel_re, kernel_im, cosine_table, sine_table):
    freq_re, freq_im = transform(real_part, imag_part, cosine_table, sine_table, 1.0)
    freq_re, freq_im = multiply(kernel_re, kernel_im, freq_re, freq_im)
    return transform(freq_re, freq_im, cosine_table, sine_table, -1.0)


def box_mean(padded):
    row_count = padded.shape[2] - 2
    col_count = padded.shape[3] - 2
    summed = jnp.zeros(padded.shape[:2] + (row_count, col_count), jnp.float32)
    for row_at in range(3):
        for col_at in range(3):
            summed = summed + padded[:, :, row_at : row_at + row_count, col_at : col_at + col_count]
    return summed / 9.0


def body(measured, positions, probe, prop_phase, object_real, object_imag):
    slices_here, tile_y, tile_x = object_real.shape
    frames_here = measured.shape[0]
    pixels = probe.shape[-1]
    half_pix = pixels // 2
    planes_count = 2 * slices_here
    row_at = lax.axis_index("row")
    col_at = lax.axis_index("col")
    full_rows = tile_y + 2 * half_pix
    full_cols = tile_x + 2 * half_pix
    stacked = jnp.stack((object_real, object_imag))
    widened = with_halo(stacked, (("row", 2), ("col", 3)), half_pix)
    planes = widened.reshape(planes_count, full_rows, full_cols)
    off_rows = positions[:, 0] - (row_at * tile_y - half_pix)
    off_cols = positions[:, 1] - (col_at * tile_x - half_pix)
    zero_index = jnp.zeros((), jnp.int32)

    def cut_one(row_off, col_off):
        return lax.dynamic_slice(
            planes, (zero_index, row_off, col_off), (planes_count, pixels, pixels)
        )

    cut_all = jax.vmap(cut_one)(off_rows, off_cols)
    cosine_table, sine_table = tables(pixels)
    kernel_re = jnp.cos(prop_phase)
    kernel_im = jnp.sin(prop_phase)
    wave_re = jnp.broadcast_to(probe[0], (frames_here, pixels, pixels))
    wave_im = jnp.broadcast_to(probe[1], (frames_here, pixels, pixels))
    waves = []
    patches = []
    exit_re, exit_im = (wave_re, wave_im)
    for slice_at in range(slices_here):
        patch_re = cut_all[:, slice_at]
        patch_im = cut_all[:, slices_here + slice_at]
        waves.append((wave_re, wave_im))
        patches.append((patch_re, patch_im))
        exit_re, exit_im = multiply(wave_re, wave_im, patch_re, patch_im)
        if slice_at < slices_here - 1:
            wave_re, wave_im = propagate(
                exit_re, exit_im, kernel_re, kernel_im, cosine_table, sine_table
            )
    far_re, far_im = transform(exit_re, exit_im, cosine_table, sine_table, 1.0)
    residual = far_re * far_re + far_im * far_im - measured
    back_re, back_im = transform(
        residual * far_re, residual * far_im, cosine_table, sine_table, -1.0
    )
    grads_re = [None] * slices_here
    grads_im = [None] * slices_here
    probe_re, probe_im = (back_re, back_im)
    for slice_at in reversed(range(slices_here)):
        grads_re[slice_at], grads_im[slice_at] = conj_multiply(
            waves[slice_at][0], waves[slice_at][1], back_re, back_im
        )
        probe_re, probe_im = conj_multiply(
            patches[slice_at][0], patches[slice_at][1], back_re, back_im
        )
        if slice_at > 0:
            back_re, back_im = propagate(
                probe_re, probe_im, kernel_re, -kernel_im, cosine_table, sine_table
            )
    probe_part = jnp.stack((jnp.sum(probe_re, axis=0), jnp.sum(probe_im, axis=0)))
    probe_total = gathered_total(probe_part, ("row", "col"))
    gradient = jnp.stack(grads_re + grads_im, axis=1)

    def place_one(frame_at, canvas_now):
        corner = (zero_index, off_rows[frame_at], off_cols[frame_at])
        previous = lax.dynamic_slice(canvas_now, corner, (planes_count, pixels, pixels))
        return lax.dynamic_update_slice(canvas_now, previous + gradient[frame_at], corner)

    canvas = lax.fori_loop(
        0, frames_here, place_one, jnp.zeros((planes_count, full_rows, full_cols), jnp.float32)
    )
    canvas = canvas.reshape(2, slices_here, full_rows, full_cols)
    top_rim = canvas[:, :, :half_pix]
    bottom_rim = canvas[:, :, half_pix + tile_y :]
    middle = canvas[:, :, half_pix : half_pix + tile_y]
    for step_by, outgoing, row_dest in ((1, bottom_rim, 0), (-1, top_rim, tile_y - half_pix)):
        received = shifted(outgoing, "row", step_by)
        middle = middle.at[:, :, row_dest : row_dest + half_pix].add(received)
    left_rim = middle[:, :, :, :half_pix]
    right_rim = middle[:, :, :, half_pix + tile_x :]
    center = middle[:, :, :, half_pix : half_pix + tile_x]
    for step_by, outgoing, col_dest in ((1, right_rim, 0), (-1, left_rim, tile_x - half_pix)):
        received = shifted(outgoing, "col", step_by)
        center = center.at[:, :, :, col_dest : col_dest + half_pix].add(received)
    smoothed = center
    whole_rows = tile_y * lax.axis_size("row")
    whole_cols = tile_x * lax.axis_size("col")
    padded = with_halo(smoothed, (("row", 2), ("col", 3)), PASSES)
    for pass_at in range(PASSES):
        padded = box_mean(padded)
        margin = PASSES - pass_at - 1
        global_rows = row_at * tile_y - margin + jnp.arange(tile_y + 2 * margin, dtype=jnp.int32)
        global_cols = col_at * tile_x - margin + jnp.arange(tile_x + 2 * margin, dtype=jnp.int32)
        inside_rows = jnp.logical_and(global_rows >= 0, global_rows < whole_rows)
        inside_cols = jnp.logical_and(global_cols >= 0, global_cols < whole_cols)
        inside = jnp.logical_and(inside_rows[:, None], inside_cols[None, :])
        padded = jnp.where(inside[None, None], padded, 0.0)
    smoothed = padded
    new_real = object_real - object_rate * smoothed[0]
    new_imag = object_imag - object_rate * smoothed[1]
    norm_scale = jnp.sqrt(jnp.mean(probe_total * probe_total) + 1e-06)
    new_probe = probe - probe_rate * probe_total / norm_scale
    return (new_real, new_imag, new_probe)


def solution(mesh):
    in_specs = (
        P(("row", "col"), None, None),
        P(("row", "col"), None),
        P(),
        P(),
        P(None, "row", "col"),
        P(None, "row", "col"),
    )
    out_specs = (P(None, "row", "col"), P(None, "row", "col"), P())
    return jax.shard_map(body, mesh=mesh, in_specs=in_specs, out_specs=out_specs, check_vma=False)
```

profile of v0, /device:TPU:18, one launch (start us, length us, event | category | flops | bytes accessed | tf_op | source)
XLA Modules:
  0.0 299.2 jit_solution(6736931437122724705)
XLA Ops:
  11.5 2.4 collective-permute-start
  14.5 3.7 %collective-permute-done.1 = f32[2,4,64,128]{2,3,1,0:T(8,128)S(1)} collective-permute-done((f32[2,4,64,128]{2,3,1,0:T(8,128)S(1)}, f32[2,4,64,128]{2,3,1,0:T(8,128)S(1)}, u32[]{:S(2)}, u32[]{:S(2)}) %collective-permute-start.1) | collective-permute-done | bytes 262176 | tf_op jit(solution)/shard_map/ppermute | solution.py:26
  18.2 3.8 %collective-permute-done = f32[2,4,64,128]{2,3,1,0:T(8,128)S(1)} collective-permute-done((f32[2,4,64,128]{2,3,1,0:T(8,128)S(1)}, f32[2,4,64,128]{2,3,1,0:T(8,128)S(1)}, u32[]{:S(2)}, u32[]{:S(2)}) %collective-permute-start) | collective-permute-done | bytes 262176 | tf_op jit(solution)/shard_map/ppermute | solution.py:24
  22.8 5.9 %collective-permute-start.3 = (f32[2,4,256,64]{2,3,1,0:T(8,128)S(1)}, f32[2,4,256,64]{2,3,1,0:T(8,128)S(1)}, u32[]{:S(2)}, u32[]{:S(2)}) collective-permute-start(f32[2,4,256,64]{2,3,1,0:T(8,128)S(1)} %get-tuple-element.224), channel_id=1, source_target_pairs={{1,0},{2,1},{3,2},{4,3},{5,4},{6,5},{7,6},{8,7},{9,8},{10,9},{11,1... | collective-permute-start | bytes 1572872 | tf_op jit(solution)/shard_map/ppermute | solution.py:26
  32.2 7.0 %collective-permute-done.3 = f32[2,4,256,64]{2,3,1,0:T(8,128)S(1)} collective-permute-done((f32[2,4,256,64]{2,3,1,0:T(8,128)S(1)}, f32[2,4,256,64]{2,3,1,0:T(8,128)S(1)}, u32[]{:S(2)}, u32[]{:S(2)}) %collective-permute-start.3) | collective-permute-done | bytes 524320 | tf_op jit(solution)/shard_map/ppermute | solution.py:26
  40.0 5.5 %collective-permute-done.2 = f32[2,4,256,64]{2,3,1,0:T(8,128)} collective-permute-done((f32[2,4,256,64]{2,3,1,0:T(8,128)S(1)}, f32[2,4,256,64]{2,3,1,0:T(8,128)}, u32[]{:S(2)}, u32[]{:S(2)}) %collective-permute-start.2) | collective-permute-done | bytes 524320 | tf_op jit(solution)/shard_map/ppermute | solution.py:24
  47.3 14.3 %while.19 = (s32[]{:T(128)}, f32[8,256,256]{1,2,0:T(8,128)S(1)}, s32[4,3]{1,0:T(4,128)S(1)}, f32[4,8,128,128]{2,3,0,1:T(8,128)}, s32[]{:T(128)}) while((s32[]{:T(128)}, f32[8,256,256]{1,2,0:T(8,128)S(1)}, s32[4,3]{1,0:T(4,128)S(1)}, f32[4,8,128,128]{2,3,0,1:T(8,128)}, s32[]{:T(128)}) %tuple.108), condition=%wide.while_cond.4, body=%wide.while_body.4.sunk | while | flops 2 | bytes 4194429 | solution.py:109
  61.6 1.9 fusion.253
  160.1 46.0 %while.18 = (s32[]{:T(128)}, f32[8,256,256]{2,1,0:T(8,128)S(1)}, s32[4]{0:T(128)S(1)}, s32[4]{0:T(128)S(1)}, f32[4,8,128,128]{2,3,0,1:T(8,128)}, /*index=5*/s32[]{:T(128)}, s32[]{:T(128)}, s32[]{:T(128)}) while((s32[]{:T(128)}, f32[8,256,256]{2,1,0:T(8,128)S(1)}, s32[4]{0:T(128)S(1)}, s32[4]{0:T(128)S(1)}, f32[4,8,128,128]{2,3,0,1:T(8,128)}, ...), condition=%wide.region_1.2_spmd, body=%wide.region_0.1_spmd.sunk | while | flops 131080 | bytes 4718793 | solution.py:160
  166.7 6.8 %dynamic_update_slice.8 = f32[8,256,256]{2,1,0:T(8,128)S(1)} dynamic-update-slice(f32[8,256,256]{2,1,0:T(8,128)S(1)} %get-tuple-element.343, f32[8,128,128]{2,1,0:T(8,128)S(1)} %bitcast_add_fusion.2, s32[]{:T(128)} %constant.191.clone.1..sunk, s32[]{:T(128)S(6)} %select_n.644, s32[]{:T(128)S(6)} %select_n.645) | dynamic-update-slice | bytes 1048580 | tf_op jit(solution)/shard_map/while/body/eval_jaxpr/dynamic_update_slice | solution.py:158
  180.1 3.1 %dynamic_update_slice.8 = f32[8,256,256]{2,1,0:T(8,128)S(1)} dynamic-update-slice(f32[8,256,256]{2,1,0:T(8,128)S(1)} %get-tuple-element.343, f32[8,128,128]{2,1,0:T(8,128)S(1)} %bitcast_add_fusion.2, s32[]{:T(128)} %constant.191.clone.1..sunk, s32[]{:T(128)S(6)} %select_n.644, s32[]{:T(128)S(6)} %select_n.645) | dynamic-update-slice | bytes 1048580 | tf_op jit(solution)/shard_map/while/body/eval_jaxpr/dynamic_update_slice | solution.py:158
  189.8 3.5 %dynamic_update_slice.8 = f32[8,256,256]{2,1,0:T(8,128)S(1)} dynamic-update-slice(f32[8,256,256]{2,1,0:T(8,128)S(1)} %get-tuple-element.343, f32[8,128,128]{2,1,0:T(8,128)S(1)} %bitcast_add_fusion.2, s32[]{:T(128)} %constant.191.clone.1..sunk, s32[]{:T(128)S(6)} %select_n.644, s32[]{:T(128)S(6)} %select_n.645) | dynamic-update-slice | bytes 1048580 | tf_op jit(solution)/shard_map/while/body/eval_jaxpr/dynamic_update_slice | solution.py:158
  199.9 6.2 %dynamic_update_slice.8 = f32[8,256,256]{2,1,0:T(8,128)S(1)} dynamic-update-slice(f32[8,256,256]{2,1,0:T(8,128)S(1)} %get-tuple-element.343, f32[8,128,128]{2,1,0:T(8,128)S(1)} %bitcast_add_fusion.2, s32[]{:T(128)} %constant.191.clone.1..sunk, s32[]{:T(128)S(6)} %select_n.644, s32[]{:T(128)S(6)} %select_n.645) | dynamic-update-slice | bytes 1048580 | tf_op jit(solution)/shard_map/while/body/eval_jaxpr/dynamic_update_slice | solution.py:158
  209.1 3.6 %collective-permute-start.5 = (f32[2,4,64,256]{3,2,1,0:T(8,128)}, f32[2,4,64,256]{3,2,1,0:T(8,128)S(1)}, u32[]{:S(2)}, u32[]{:S(2)}) collective-permute-start(f32[2,4,64,256]{3,2,1,0:T(8,128)} %get-tuple-element.219), channel_id=1, source_target_pairs={{16,0},{32,16},{48,32},{64,48},{80,64},{96,80},{112,96},{17,1},{33... | collective-permute-start | bytes 1572872 | tf_op jit(solution)/shard_map/ppermute | solution.py:40
  213.0 16.3 %collective-permute-done.4 = f32[2,4,64,256]{3,2,1,0:T(8,128)S(1)} collective-permute-done((f32[2,4,64,256]{3,2,1,0:T(8,128)}, f32[2,4,64,256]{3,2,1,0:T(8,128)S(1)}, u32[]{:S(2)}, u32[]{:S(2)}) %collective-permute-start.4) | collective-permute-done | bytes 524320 | tf_op jit(solution)/shard_map/ppermute | solution.py:40
  233.6 6.0 %collective-permute-start.7 = (f32[2,4,128,64]{3,2,1,0:T(8,128)S(1)}, f32[2,4,128,64]{3,2,1,0:T(8,128)S(1)}, u32[]{:S(2)}, u32[]{:S(2)}) collective-permute-start(f32[2,4,128,64]{3,2,1,0:T(8,128)S(1)} %get-tuple-element.221), channel_id=1, source_target_pairs={{1,0},{2,1},{3,2},{4,3},{5,4},{6,5},{7,6},{8,7},{9,8},{10,9},{11,1... | collective-permute-start | bytes 786440 | tf_op jit(solution)/shard_map/ppermute | solution.py:40
  239.6 8.7 %collective-permute-done.6 = f32[2,4,128,64]{3,2,1,0:T(8,128)S(1)} collective-permute-done((f32[2,4,128,64]{3,2,1,0:T(8,128)S(1)}, f32[2,4,128,64]{3,2,1,0:T(8,128)S(1)}, u32[]{:S(2)}, u32[]{:S(2)}) %collective-permute-start.6) | collective-permute-done | bytes 262176 | tf_op jit(solution)/shard_map/ppermute | solution.py:40
  250.0 2.6 scatter-add.19
  252.6 4.6 %collective-permute-start.9 = (f32[2,4,3,128]{3,2,1,0:T(4,128)S(1)}, f32[2,4,3,128]{3,2,1,0:T(4,128)S(1)}, u32[]{:S(2)}, u32[]{:S(2)}) collective-permute-start(f32[2,4,3,128]{3,2,1,0:T(4,128)S(1)} %get-tuple-element.230), channel_id=1, source_target_pairs={{16,0},{32,16},{48,32},{64,48},{80,64},{96,80},{112,96},{17,1},{33... | collective-permute-start | bytes 36872 | tf_op jit(solution)/shard_map/ppermute | solution.py:26
  259.2 3.1 %collective-permute-done.8 = f32[2,4,3,128]{3,2,1,0:T(4,128)S(1)} collective-permute-done((f32[2,4,3,128]{3,2,1,0:T(4,128)S(1)}, f32[2,4,3,128]{3,2,1,0:T(4,128)S(1)}, u32[]{:S(2)}, u32[]{:S(2)}) %collective-permute-start.8) | collective-permute-done | bytes 12320 | tf_op jit(solution)/shard_map/ppermute | solution.py:24
  262.9 6.2 %collective-permute-start.11 = (f32[2,4,134,3]{2,1,3,0:T(4,128)S(1)}, f32[2,4,134,3]{2,1,3,0:T(4,128)S(1)}, u32[]{:S(2)}, u32[]{:S(2)}) collective-permute-start(f32[2,4,134,3]{2,1,3,0:T(4,128)S(1)} %copy.537), channel_id=1, source_target_pairs={{1,0},{2,1},{3,2},{4,3},{5,4},{6,5},{7,6},{8,7},{9,8},{10,9},{11,1... | collective-permute-start | bytes 38600 | tf_op jit(solution)/shard_map/ppermute | solution.py:26
  269.4 2.1 collective-permute-start.10
  271.9 5.4 %collective-permute-done.10 = f32[2,4,134,3]{2,1,3,0:T(4,128)S(1)} collective-permute-done((f32[2,4,134,3]{2,1,3,0:T(4,128)S(1)}, f32[2,4,134,3]{2,1,3,0:T(4,128)S(1)}, u32[]{:S(2)}, u32[]{:S(2)}) %collective-permute-start.10) | collective-permute-done | bytes 12896 | tf_op jit(solution)/shard_map/ppermute | solution.py:24
  283.5 6.6 %reduce_sum.38 = f32[2,128,128]{2,1,0:T(8,128)S(1)} reduce(f32[128,2,128,128]{3,2,1,0:T(8,128)} %bitcast.550, f32[]{:T(128)} %constant.197.clone.1), dimensions={0}, to_apply=%region_4.5 | reduce | flops 4161536 | bytes 16908292 | tf_op jit(solution)/shard_map/reduce_sum | solution.py:34
  (255 shorter events, 151.9 us)
Async XLA Ops:
  7.2 6.8 %copy-start.11 = (f32[128,128]{1,0:T(8,128)S(1)}, f32[128,128]{1,0:T(8,128)}, u32[]{:S(2)}) copy-start(f32[128,128]{1,0:T(8,128)} %param.19) | copy-start | bytes 196612
  7.2 7.2 %copy-start.12 = (s32[4,2]{0,1:T(2,128)S(1)}, s32[4,2]{0,1:T(2,128)}, u32[]{:S(2)}) copy-start(s32[4,2]{0,1:T(2,128)} %param.17) | copy-start | bytes 100
  7.2 276.3 %all-gather.3.cloned.1.call-start = ((), (), s32[]{:S(2)}) async-start(), calls=%async_computation | async-start | bytes 16908288 | tf_op jit(solution)/shard_map/all_gather | solution.py:34
  9.6 8.6 %collective-permute-start.1 = (f32[2,4,64,128]{2,3,1,0:T(8,128)S(1)}, f32[2,4,64,128]{2,3,1,0:T(8,128)S(1)}, u32[]{:S(2)}, u32[]{:S(2)}) collective-permute-start(f32[2,4,64,128]{2,3,1,0:T(8,128)S(1)} %get-tuple-element.232), channel_id=1, source_target_pairs={{16,0},{32,16},{48,32},{64,48},{80,64},{96,80},{112,96},{17,1},{33... | collective-permute-start | bytes 786440 | tf_op jit(solution)/shard_map/ppermute | solution.py:26
  11.5 10.5 %collective-permute-start = (f32[2,4,64,128]{2,3,1,0:T(8,128)S(1)}, f32[2,4,64,128]{2,3,1,0:T(8,128)S(1)}, u32[]{:S(2)}, u32[]{:S(2)}) collective-permute-start(f32[2,4,64,128]{2,3,1,0:T(8,128)S(1)} %get-tuple-element.231), channel_id=1, source_target_pairs={{0,16},{16,32},{32,48},{48,64},{64,80},{80,96},{96,112},{1,17},{17... | collective-permute-start | bytes 786440 | tf_op jit(solution)/shard_map/ppermute | solution.py:24
  14.5 16.1 %copy-start.8 = (f32[2,128,128]{2,1,0:T(8,128)S(1)}, f32[2,128,128]{2,1,0:T(8,128)}, u32[]{:S(2)}) copy-start(f32[2,128,128]{2,1,0:T(8,128)} %param.18) | copy-start | bytes 393220
  14.5 16.5 %copy-start.10 = (f32[4,128,128]{2,1,0:T(8,128)S(1)}, f32[4,128,128]{2,1,0:T(8,128)}, u32[]{:S(2)}) copy-start(f32[4,128,128]{2,1,0:T(8,128)} %param.16) | copy-start | bytes 786436
  22.8 16.3 %collective-permute-start.3 = (f32[2,4,256,64]{2,3,1,0:T(8,128)S(1)}, f32[2,4,256,64]{2,3,1,0:T(8,128)S(1)}, u32[]{:S(2)}, u32[]{:S(2)}) collective-permute-start(f32[2,4,256,64]{2,3,1,0:T(8,128)S(1)} %get-tuple-element.224), channel_id=1, source_target_pairs={{1,0},{2,1},{3,2},{4,3},{5,4},{6,5},{7,6},{8,7},{9,8},{10,9},{11,1... | collective-permute-start | bytes 1572872 | tf_op jit(solution)/shard_map/ppermute | solution.py:26
  28.7 16.7 %collective-permute-start.2 = (f32[2,4,256,64]{2,3,1,0:T(8,128)S(1)}, f32[2,4,256,64]{2,3,1,0:T(8,128)}, u32[]{:S(2)}, u32[]{:S(2)}) collective-permute-start(f32[2,4,256,64]{2,3,1,0:T(8,128)S(1)} %get-tuple-element.223), channel_id=1, source_target_pairs={{0,1},{1,2},{2,3},{3,4},{4,5},{5,6},{6,7},{7,8},{8,9},{9,10},{10,1... | collective-permute-start | bytes 1572872 | tf_op jit(solution)/shard_map/ppermute | solution.py:24
  39.1 0.8 copy-start.7
  61.6 6.3 %copy-start.1 = (f32[4,8,128,128]{2,3,0,1:T(8,128)S(1)}, f32[4,8,128,128]{2,3,0,1:T(8,128)}, u32[]{:S(2)}) copy-start(f32[4,8,128,128]{2,3,0,1:T(8,128)} %get-tuple-element.153) | copy-start | bytes 6291460
  102.8 4.4 %copy-start = (f32[4,128,128]{1,2,0:T(8,128)S(1)}, f32[4,128,128]{1,2,0:T(8,128)}, u32[]{:S(2)}) copy-start(f32[4,128,128]{1,2,0:T(8,128)} %copy.477) | copy-start | bytes 786436
  154.4 3.2 %copy-start.2 = (f32[4,128,128]{1,2,0:T(8,128)S(1)}, f32[4,128,128]{1,2,0:T(8,128)}, u32[]{:S(2)}) copy-start(f32[4,128,128]{1,2,0:T(8,128)} %get-tuple-element.248) | copy-start | bytes 786436
  207.2 22.1 %collective-permute-start.4 = (f32[2,4,64,256]{3,2,1,0:T(8,128)}, f32[2,4,64,256]{3,2,1,0:T(8,128)S(1)}, u32[]{:S(2)}, u32[]{:S(2)}) collective-permute-start(f32[2,4,64,256]{3,2,1,0:T(8,128)} %get-tuple-element.220), channel_id=1, source_target_pairs={{0,16},{16,32},{32,48},{48,64},{64,80},{80,96},{96,112},{1,17},{17... | collective-permute-start | bytes 1572872 | tf_op jit(solution)/shard_map/ppermute | solution.py:40
  209.1 21.9 %collective-permute-start.5 = (f32[2,4,64,256]{3,2,1,0:T(8,128)}, f32[2,4,64,256]{3,2,1,0:T(8,128)S(1)}, u32[]{:S(2)}, u32[]{:S(2)}) collective-permute-start(f32[2,4,64,256]{3,2,1,0:T(8,128)} %get-tuple-element.219), channel_id=1, source_target_pairs={{16,0},{32,16},{48,32},{64,48},{80,64},{96,80},{112,96},{17,1},{33... | collective-permute-start | bytes 1572872 | tf_op jit(solution)/shard_map/ppermute | solution.py:40
  231.4 17.0 %collective-permute-start.6 = (f32[2,4,128,64]{3,2,1,0:T(8,128)S(1)}, f32[2,4,128,64]{3,2,1,0:T(8,128)S(1)}, u32[]{:S(2)}, u32[]{:S(2)}) collective-permute-start(f32[2,4,128,64]{3,2,1,0:T(8,128)S(1)} %get-tuple-element.222), channel_id=1, source_target_pairs={{0,1},{1,2},{2,3},{3,4},{4,5},{5,6},{6,7},{7,8},{8,9},{9,10},{10,1... | collective-permute-start | bytes 786440 | tf_op jit(solution)/shard_map/ppermute | solution.py:40
  233.6 16.2 %collective-permute-start.7 = (f32[2,4,128,64]{3,2,1,0:T(8,128)S(1)}, f32[2,4,128,64]{3,2,1,0:T(8,128)S(1)}, u32[]{:S(2)}, u32[]{:S(2)}) collective-permute-start(f32[2,4,128,64]{3,2,1,0:T(8,128)S(1)} %get-tuple-element.221), channel_id=1, source_target_pairs={{1,0},{2,1},{3,2},{4,3},{5,4},{6,5},{7,6},{8,7},{9,8},{10,9},{11,1... | collective-permute-start | bytes 786440 | tf_op jit(solution)/shard_map/ppermute | solution.py:40
  252.6 6.5 %collective-permute-start.9 = (f32[2,4,3,128]{3,2,1,0:T(4,128)S(1)}, f32[2,4,3,128]{3,2,1,0:T(4,128)S(1)}, u32[]{:S(2)}, u32[]{:S(2)}) collective-permute-start(f32[2,4,3,128]{3,2,1,0:T(4,128)S(1)} %get-tuple-element.230), channel_id=1, source_target_pairs={{16,0},{32,16},{48,32},{64,48},{80,64},{96,80},{112,96},{17,1},{33... | collective-permute-start | bytes 36872 | tf_op jit(solution)/shard_map/ppermute | solution.py:26
  257.2 5.1 %collective-permute-start.8 = (f32[2,4,3,128]{3,2,1,0:T(4,128)S(1)}, f32[2,4,3,128]{3,2,1,0:T(4,128)S(1)}, u32[]{:S(2)}, u32[]{:S(2)}) collective-permute-start(f32[2,4,3,128]{3,2,1,0:T(4,128)S(1)} %get-tuple-element.229), channel_id=1, source_target_pairs={{0,16},{16,32},{32,48},{48,64},{64,80},{80,96},{96,112},{1,17},{17... | collective-permute-start | bytes 36872 | tf_op jit(solution)/shard_map/ppermute | solution.py:24
  262.9 8.7 %collective-permute-start.11 = (f32[2,4,134,3]{2,1,3,0:T(4,128)S(1)}, f32[2,4,134,3]{2,1,3,0:T(4,128)S(1)}, u32[]{:S(2)}, u32[]{:S(2)}) collective-permute-start(f32[2,4,134,3]{2,1,3,0:T(4,128)S(1)} %copy.537), channel_id=1, source_target_pairs={{1,0},{2,1},{3,2},{4,3},{5,4},{6,5},{7,6},{8,7},{9,8},{10,9},{11,1... | collective-permute-start | bytes 38600 | tf_op jit(solution)/shard_map/ppermute | solution.py:26
  269.4 7.8 %collective-permute-start.10 = (f32[2,4,134,3]{2,1,3,0:T(4,128)S(1)}, f32[2,4,134,3]{2,1,3,0:T(4,128)S(1)}, u32[]{:S(2)}, u32[]{:S(2)}) collective-permute-start(f32[2,4,134,3]{2,1,3,0:T(4,128)S(1)} %copy.536), channel_id=1, source_target_pairs={{0,1},{1,2},{2,3},{3,4},{4,5},{5,6},{6,7},{7,8},{8,9},{9,10},{10,1... | collective-permute-start | bytes 38600 | tf_op jit(solution)/shard_map/ppermute | solution.py:24
  281.6 1.0 copy-start.5
  281.7 1.0 copy-start.6
  283.5 7.9 %copy-start.9 = (f32[2,128,128]{2,1,0:T(8,128)S(1)}, f32[2,128,128]{2,1,0:T(8,128)}, u32[]{:S(2)}) copy-start(f32[2,128,128]{2,1,0:T(8,128)} %param.18) | copy-start | bytes 393220
  (2 other events, 1.5 us)
Sparse Core Ops, SparseCore 0:
  152.9 81.5 all-gather.2
where the time goes:
time: 303 us; the launch traced here: 299 us
  matrix products  88.8 us (29%)
  local copies, waits for them, and re-layouts  56.6 us (19%)
  waiting for transfers between devices  55.4 us (18%)
  starting transfers between devices  40.5 us (13%)
  other arithmetic  25.6 us (8%)
  between operations  16.3 us (5%)
  loops' own time  16.1 us (5%)
    ppermute x4, waiting for transfers between devices, shifted(): return lax.ppermute(value, axis, pairs)  26.9 us
    dynamic_update_slice x4, local copies, waits for them, and re-layouts, place_one(): lax.dynamic_update_slice(canvas_now, previous + gradient[frame_at], corner)  19.5 us
    ppermute x4, starting transfers between devices, with_halo(): lax.ppermute(head, axis, [((i + 1) % count, i) for i in range(ends)])  18.6 us
    ppermute x4, waiting for transfers between devices, with_halo(): lax.ppermute(tail, axis, [(i, (i + 1) % count) for i in range(ends)])  17.8 us
    another operation x1, loops' own time, body(): lax.fori_loop(0, frames_here, place_one, jnp.zeros((planes_count, full_ro...  15.7 us
    gather x24, local copies, waits for them, and re-layouts  13.9 us
    ppermute x4, starting transfers between devices, shifted(): return lax.ppermute(value, axis, pairs)  13.5 us
    dot_general x14, matrix products, transform(): jnp.einsum('lj,fjk->flk', sine_table, right_re, precision=highest)  12.5 us
  transfers between devices with their start and end apart: 13, of which 10 were waited for; matrix products, arithmetic and copies ran while one was open for 18% of the time, Pallas kernels for 0%

commit v1 on v0

v1 whole, which is shorter than its diff:
```python
import math

import numpy as np
import jax
import jax.numpy as jnp
from jax import lax
from jax.experimental import pallas as pl
from jax.experimental.pallas import tpu as pltpu
from jax.sharding import PartitionSpec as P

PIX = 128
HALF = 64
SL = 4
NP_ = 2 * SL
RIM = 72
F32 = jnp.float32
BF16 = jnp.bfloat16
AXES = ("row", "col")

object_rate = 0.5
probe_rate = 0.5


def dft_tables():
    counter = np.arange(PIX)
    angles = (counter[:, None] * counter[None, :] % PIX) * (2.0 * math.pi / PIX)
    cosine = np.cos(angles) / math.sqrt(PIX)
    sine = np.sin(angles) / math.sqrt(PIX)
    first = np.block([[cosine, -sine], [sine, cosine]]).astype(np.float32)
    high = np.asarray(first.astype(jnp.bfloat16))
    low = np.asarray((first - high.astype(np.float32)).astype(jnp.bfloat16))
    return np.stack([high, low, high.T, low.T])


def split(value):
    high = value.astype(BF16)
    low = (value - high.astype(F32)).astype(BF16)
    return high, low


def mm(left, right):
    return lax.dot_general(left, right, (((1,), (0,)), ((), ())), preferred_element_type=F32)


def mm_t(left, right):
    return lax.dot_general(left, right, (((1,), (1,)), ((), ())), preferred_element_type=F32)


def lane_of(shape):
    return lax.broadcasted_iota(jnp.int32, shape, 1)


def weights(delta):
    size = jnp.abs(delta)
    return jnp.where(
        size == 0, 7.0, jnp.where(size == 1, 6.0, jnp.where(size == 2, 3.0, jnp.where(size == 3, 1.0, 0.0)))
    ).astype(F32)


def smoothing(out_at, in_at, whole):
    inner = weights(out_at - in_at) - weights(out_at + in_at + 2) - weights(out_at + in_at - 2 * whole)
    return jnp.where(jnp.logical_and(out_at >= 0, out_at < whole), inner, 0.0)


def pack_kernel(real_ref, imag_ref, left_ref, right_ref):
    low = lane_of((HALF, PIX)) < HALF
    for plane in range(NP_):
        ref = real_ref if plane < SL else imag_ref
        top = ref[plane % SL, :HALF, :]
        bottom = ref[plane % SL, HALF:, :]
        left_ref[plane] = jnp.where(low, top, pltpu.roll(bottom, HALF, 1))
        right_ref[plane] = jnp.where(low, pltpu.roll(top, HALF, 1), bottom)


def join_kernel(real_ref, imag_ref, from_left_ref, from_right_ref, top_ref, bottom_ref):
    low = lane_of((HALF, PIX)) < HALF
    for plane in range(NP_):
        ref = real_ref if plane < SL else imag_ref
        for part, out_ref in ((0, top_ref), (1, bottom_ref)):
            own = pltpu.roll(ref[plane % SL, part * HALF : (part + 1) * HALF, :], HALF, 1)
            near = from_left_ref[plane]
            far = from_right_ref[plane]
            if part == 0:
                far = pltpu.roll(far, HALF, 1)
            else:
                near = pltpu.roll(near, HALF, 1)
            out_ref[plane, 0] = jnp.where(low, near, own)
            out_ref[plane, 1] = jnp.where(low, own, far)


def main_kernel(
    at_ref, up_ref, top_ref, bottom_ref, down_ref, measured_ref, probe_ref, kernel_ref, table_ref,
    up_out, down_out, mid_out, keep_out, send_out, window, patches, waves, grads,
):
    frames = measured_ref.shape[0]
    pairs = frames // 2
    for plane in range(NP_):
        for half in range(2):
            window[plane, half, 0:64] = up_ref[plane, half]
            window[plane, half, 64:128] = top_ref[plane, half]
            window[plane, half, 128:192] = bottom_ref[plane, half]
            window[plane, half, 192:256] = down_ref[plane, half]
    lane = lane_of((PIX, PIX))

    def cut(frame, slice_at):
        row_off = at_ref[2 * frame]
        col_off = at_ref[2 * frame + 1]
        turn = lax.rem(PIX - col_off, PIX)
        near = lane < PIX - col_off
        for plane in (slice_at, SL + slice_at):
            first = pltpu.roll(window[plane, 0, pl.ds(row_off, PIX), :], turn, 1)
            second = pltpu.roll(window[plane, 1, pl.ds(row_off, PIX), :], turn, 1)
            patches[frame, plane] = jnp.where(near, first, second)

    def right(pair, which):
        rows = [jnp.concatenate([re, im], axis=1) for re, im in pair]
        high, low = split(jnp.concatenate(rows, axis=0))
        table_high = table_ref[which]
        table_low = table_ref[which + 1]
        out = mm(high, table_high) + mm(high, table_low) + mm(low, table_high)
        return [(out[i * PIX : (i + 1) * PIX, :PIX], out[i * PIX : (i + 1) * PIX, PIX:]) for i in range(2)]

    def left(pair, which):
        value = jnp.concatenate(
            [jnp.concatenate([pair[0][k], pair[1][k]], axis=1) for k in range(2)], axis=0
        )
        high, low = split(value)
        table_high = table_ref[which]
        table_low = table_ref[which + 1]
        out = mm(table_high, high) + mm(table_low, high) + mm(table_high, low)
        return [(out[:PIX, i * PIX : (i + 1) * PIX], out[PIX:, i * PIX : (i + 1) * PIX]) for i in range(2)]

    def forward(items):
        items = [right(pair, 0) for pair in items]
        return [left(pair, 2) for pair in items]

    def inverse(items):
        items = [right(pair, 2) for pair in items]
        return [left(pair, 0) for pair in items]

    def each(items, fn):
        return [[fn(2 * p + i, *items[p][i]) for i in range(2)] for p in range(pairs)]

    def times(a_re, a_im, b_re, b_im):
        return a_re * b_re - a_im * b_im, a_re * b_im + a_im * b_re

    def conj_times(a_re, a_im, b_re, b_im):
        return a_re * b_re + a_im * b_im, a_re * b_im - a_im * b_re

    def through(frame, re, im):
        return times(kernel_ref[0], kernel_ref[1], re, im)

    def through_back(frame, re, im):
        return conj_times(kernel_ref[0], kernel_ref[1], re, im)

    def wave_of(frame, slice_at):
        if slice_at == 0:
            return probe_ref[0], probe_ref[1]
        return waves[slice_at - 1, frame, 0], waves[slice_at - 1, frame, 1]

    for slice_at in range(SL):
        for frame in range(frames):
            cut(frame, slice_at)

        def exit_of(frame, *unused, slice_at=slice_at):
            wave_re, wave_im = wave_of(frame, slice_at)
            return times(wave_re, wave_im, patches[frame, slice_at], patches[frame, SL + slice_at])

        items = each([[(), ()] for _ in range(pairs)], exit_of)
        items = forward(items)
        if slice_at < SL - 1:
            items = inverse(each(items, through))
            for p in range(pairs):
                for i in range(2):
                    waves[slice_at, 2 * p + i, 0] = items[p][i][0]
                    waves[slice_at, 2 * p + i, 1] = items[p][i][1]

    def residual_of(frame, re, im):
        residual = re * re + im * im - measured_ref[frame]
        return residual * re, residual * im

    back = inverse(each(items, residual_of))
    for slice_at in reversed(range(SL)):

        def emit(frame, re, im, slice_at=slice_at):
            wave_re, wave_im = wave_of(frame, slice_at)
            term_re, term_im = conj_times(wave_re, wave_im, re, im)
            grads[slice_at, frame] = term_re
            grads[SL + slice_at, frame] = term_im
            return conj_times(patches[frame, slice_at], patches[frame, SL + slice_at], re, im)

        back = each(back, emit)
        if slice_at > 0:
            back = inverse(each(forward(back), through_back))

    sums = []
    for k in range(2):
        total = back[0][0][k] + back[0][1][k]
        for p in range(1, pairs):
            total = total + (back[p][0][k] + back[p][1][k])
        sums.append(total)
    first_core = at_ref[8] == 0
    keep_out[...] = jnp.where(first_core, sums[0], sums[1])
    send_out[...] = jnp.where(first_core, sums[1], sums[0])

    row_base = at_ref[9]
    whole_rows = at_ref[10]
    shape = (256 + 16, PIX)
    out_at = lax.broadcasted_iota(jnp.int32, shape, 0) + (row_base - 8)
    in_at = lax.broadcasted_iota(jnp.int32, shape, 1) + row_base
    places = []
    for p in range(pairs):
        places.append(
            jnp.concatenate(
                [smoothing(out_at, in_at + at_ref[2 * (2 * p + i)], whole_rows) for i in range(2)], axis=1
            ).astype(BF16)
        )

    def place(plane, carry):
        out = None
        for p in range(pairs):
            rows = []
            for i in range(2):
                col_off = at_ref[2 * (2 * p + i) + 1]
                moved = pltpu.roll(grads[plane, 2 * p + i], lax.rem(col_off, PIX), 1)
                rows.append(
                    jnp.concatenate(
                        [jnp.where(lane >= col_off, moved, 0.0), jnp.where(lane < col_off, moved, 0.0)], axis=1
                    )
                )
            high, low = split(jnp.concatenate(rows, axis=0))
            part = mm(places[p], high) + mm(places[p], low)
            out = part if out is None else out + part
        for half in range(2):
            piece = out[:, half * PIX : (half + 1) * PIX]
            up_out[plane, half] = piece[0:RIM]
            mid_out[plane, half] = piece[RIM : RIM + PIX]
            down_out[plane, half] = piece[RIM + PIX :]
        return carry

    lax.fori_loop(0, NP_, place, 0)


def column_kernel(at_ref, mid_ref, from_up_ref, from_down_ref, left_out, right_out, center_out):
    col_base = at_ref[11]
    whole_cols = at_ref[12]
    shape = (256 + 16, 256)
    out_at = lax.broadcasted_iota(jnp.int32, shape, 0) + (col_base - 8)
    in_at = lax.broadcasted_iota(jnp.int32, shape, 1) + col_base
    table = smoothing(out_at, in_at, whole_cols).astype(BF16)
    for first in range(0, NP_, 2):
        rows = []
        for plane in (first, first + 1):
            halves = []
            for half in range(2):
                value = mid_ref[plane, half]
                add_top = from_up_ref[plane, half]
                add_low = from_down_ref[plane, half]
                halves.append(
                    jnp.concatenate(
                        [
                            value[:56] + add_top[:56],
                            value[56:RIM] + add_top[56:] + add_low[: RIM - 56],
                            value[RIM:] + add_low[RIM - 56 :],
                        ],
                        axis=0,
                    )
                )
            rows.append(jnp.concatenate(halves, axis=1))
        high, low = split(jnp.concatenate(rows, axis=0))
        out = mm_t(table, high) + mm_t(table, low)
        for i in range(2):
            piece = out[:, i * PIX : (i + 1) * PIX]
            left_out[first + i] = piece[0:RIM]
            center_out[first + i] = piece[RIM : RIM + PIX]
            right_out[first + i] = piece[RIM + PIX :]


def final_kernel(real_ref, imag_ref, center_ref, from_left_ref, from_right_ref, real_out, imag_out):
    scale = object_rate / 729.0
    for plane in range(NP_):
        value = center_ref[plane]
        add_low = from_left_ref[plane]
        add_high = from_right_ref[plane]
        total = jnp.concatenate(
            [
                value[:56] + add_low[:56],
                value[56:RIM] + add_low[56:] + add_high[: RIM - 56],
                value[RIM:] + add_high[RIM - 56 :],
            ],
            axis=0,
        )
        ref, out = (real_ref, real_out) if plane < SL else (imag_ref, imag_out)
        out[plane % SL] = ref[plane % SL] - scale * total.T


def probe_kernel(at_ref, own_ref, other_ref, probe_ref, out_ref):
    first_core = at_ref[8] == 0
    own = own_ref[...]
    other = other_ref[...]
    real = jnp.where(first_core, own, other)
    imag = jnp.where(first_core, other, own)
    mean = jnp.sum(real * real + imag * imag, keepdims=True) / (2.0 * PIX * PIX)
    scale = jnp.sqrt(mean + 1e-06)
    out_ref[0] = probe_ref[0] - probe_rate * real / scale
    out_ref[1] = probe_ref[1] - probe_rate * imag / scale


VMEM = pl.BlockSpec(memory_space=pltpu.VMEM)
SMEM = pl.BlockSpec(memory_space=pltpu.SMEM)


def call(fn, shapes, smem=0, scratch=(), flops=1_000_000):
    def run(*args):
        specs = [SMEM] * smem + [VMEM] * (len(args) - smem)
        return pl.pallas_call(
            fn,
            out_shape=[jax.ShapeDtypeStruct(s, F32) for s in shapes],
            in_specs=specs,
            out_specs=[VMEM] * len(shapes),
            scratch_shapes=list(scratch),
            cost_estimate=pl.CostEstimate(flops=flops, bytes_accessed=1_000_000, transcendentals=0),
            compiler_params=pltpu.CompilerParams(vmem_limit_bytes=60 * 1024 * 1024),
            name=fn.__name__,
        )(*args)

    return run


def turned(value, axis, by):
    count = lax.axis_size(axis)
    return lax.ppermute(value, axis, [(i, (i + by) % count) for i in range(count)])


def ring_of(axis, count, of, to):
    return [(i, to(i)) for i in range(count)]


def ring_total(value, axis, low, size):
    count = lax.axis_size(axis)

    def by(step):
        pairs = []
        for i in range(count):
            digit = i // low % size
            pairs.append((i, i + ((digit + step) % size - digit) * low))
        return lax.ppermute(value, axis, pairs)

    next_one, before, across = by(1), by(3), by(2)
    return (value + across) + (next_one + before)


def core_swap(value):
    count = lax.axis_size("row")
    return lax.ppermute(value, "row", [(i, i ^ 1) for i in range(count)])


def body(measured, positions, probe, prop_phase, object_real, object_imag):
    row_at = lax.axis_index("row")
    col_at = lax.axis_index("col")
    frames = measured.shape[0]
    base = jnp.stack([row_at * PIX - HALF, col_at * PIX - HALF]).astype(jnp.int32)
    offsets = (positions - base[None, :]).reshape(-1)
    extra = jnp.stack(
        [
            row_at % 2,
            base[0],
            jnp.int32(PIX * lax.axis_size("row")),
            base[1],
            jnp.int32(PIX * lax.axis_size("col")),
        ]
    ).astype(jnp.int32)
    at = jnp.concatenate([offsets, extra])

    face = (NP_, HALF, PIX)
    left_send, right_send = call(pack_kernel, [face, face])(object_real, object_imag)
    from_left = turned(right_send, "col", 1)
    from_right = turned(left_send, "col", -1)
    band = (NP_, 2, HALF, PIX)
    top, bottom = call(join_kernel, [band, band])(object_real, object_imag, from_left, from_right)
    up = turned(bottom, "row", 1)
    down = turned(top, "row", -1)
    kernel = jnp.stack([jnp.cos(prop_phase), jnp.sin(prop_phase)])
    tables = jnp.asarray(dft_tables())
    rim = (NP_, 2, RIM, PIX)
    flat = (PIX, PIX)
    up_send, down_send, middle, keep, send = call(
        main_kernel,
        [rim, rim, (NP_, 2, PIX, PIX), flat, flat],
        smem=1,
        scratch=[
            pltpu.VMEM((NP_, 2, 256, PIX), F32),
            pltpu.VMEM((frames, NP_, PIX, PIX), F32),
            pltpu.VMEM((SL - 1, frames, 2, PIX, PIX), F32),
            pltpu.VMEM((NP_, frames, PIX, PIX), F32),
        ],
        flops=12_000_000_000,
    )(at, up, top, bottom, down, measured, probe, kernel, tables)
    from_up = turned(down_send, "row", 1)
    from_down = turned(up_send, "row", -1)
    side = (NP_, RIM, PIX)
    left_out, right_out, center = call(column_kernel, [side, side, (NP_, PIX, PIX)], smem=1)(
        at, middle, from_up, from_down
    )
    side_left = turned(right_out, "col", 1)
    side_right = turned(left_out, "col", -1)
    tile = (SL, PIX, PIX)
    new_real, new_imag = call(final_kernel, [tile, tile])(
        object_real, object_imag, center, side_left, side_right
    )

    half_sum = keep + core_swap(send)
    half_sum = ring_total(half_sum, "col", 4, 4)
    half_sum = ring_total(half_sum, "col", 1, 4)
    half_sum = ring_total(half_sum, "row", 2, 4)
    other = core_swap(half_sum)
    (new_probe,) = call(probe_kernel, [(2, PIX, PIX)], smem=1)(at, half_sum, other, probe)
    return (new_real, new_imag, new_probe)


def solution(mesh):
    in_specs = (
        P(("row", "col"), None, None),
        P(("row", "col"), None),
        P(),
        P(),
        P(None, "row", "col"),
        P(None, "row", "col"),
    )
    out_specs = (P(None, "row", "col"), P(None, "row", "col"), P())
    return jax.shard_map(body, mesh=mesh, in_specs=in_specs, out_specs=out_specs, check_vma=False)
```

time: 303 us -> 91.6 us (0.30)
  the two profiles are of different devices: /device:TPU:18 before, /device:TPU:8 now
where the time goes in v1:
time: 91.6 us; the launch traced here: 91.3 us
  starting transfers between devices  29.8 us (33%)
  Pallas kernels  29.5 us (32%)
  waiting for transfers between devices  23 us (25%)
  local copies, waits for them, and re-layouts  6.54 us (7%)
  other arithmetic  1.71 us (2%)
    pallas_call x6, Pallas kernels, run(): pl.pallas_call(fn, out_shape=[jax.ShapeDtypeStruct(s, F32) for s in shape...  29.5 us
    ppermute x8, starting transfers between devices, turned(): lax.ppermute(value, axis, [(i, (i + by) % count) for i in range(count)])  15.1 us
    ppermute x9, starting transfers between devices, by(): return lax.ppermute(value, axis, pairs)  13.7 us
    ppermute x8, waiting for transfers between devices, turned(): lax.ppermute(value, axis, [(i, (i + by) % count) for i in range(count)])  12.7 us
    ppermute x9, waiting for transfers between devices, by(): return lax.ppermute(value, axis, pairs)  7.89 us
    unnamed x24, local copies, waits for them, and re-layouts  5.43 us
    ppermute x2, waiting for transfers between devices, core_swap(): return lax.ppermute(value, 'row', [(i, i ^ 1) for i in range(count)])  2.35 us
  transfers between devices with their start and end apart: 19, of which 9 were waited for; matrix products, arithmetic and copies ran while one was open for 2% of the time, Pallas kernels for 6%

profile of v1, /device:TPU:8, one launch (start us, length us, event | category | flops | bytes accessed | tf_op | source)
XLA Modules:
  0.0 91.3 jit_solution(5169773503803715103)
XLA Ops:
  0.6 2.0 %pack_kernel.1 = (f32[8,64,128]{2,1,0:T(8,128)}, f32[8,64,128]{2,1,0:T(8,128)}) custom-call(f32[4,128,128]{2,1,0:T(8,128)} %real_ref.5, f32[4,128,128]{2,1,0:T(8,128)} %imag_ref.5), custom_call_target="tpu_custom_call" | custom-call | flops 1000000 | bytes 1000000 | tf_op jit(solution)/shard_map/pack_kernel/pallas_call | solution.py:316
  2.6 1.9 %collective-permute-start = (f32[8,64,128]{2,1,0:T(8,128)}, f32[8,64,128]{2,1,0:T(8,128)S(1)}, u32[]{:S(2)}, u32[]{:S(2)}) collective-permute-start(f32[8,64,128]{2,1,0:T(8,128)} %get-tuple-element.17), channel_id=1, source_target_pairs={{0,1},{1,2},{2,3},{3,4},{4,5},{5,6},{6,7},{7,8},{8,9},{9,10},{10,1... | collective-permute-start | bytes 786440 | tf_op jit(solution)/shard_map/ppermute | solution.py:332
  4.6 4.3 %collective-permute-start.1 = (f32[8,64,128]{2,1,0:T(8,128)}, f32[8,64,128]{2,1,0:T(8,128)S(1)}, u32[]{:S(2)}, u32[]{:S(2)}) collective-permute-start(f32[8,64,128]{2,1,0:T(8,128)} %get-tuple-element.18), channel_id=1, source_target_pairs={{0,15},{1,0},{2,1},{3,2},{4,3},{5,4},{6,5},{7,6},{8,7},{9,8},{10,9... | collective-permute-start | bytes 786440 | tf_op jit(solution)/shard_map/ppermute | solution.py:332
  9.0 6.4 %collective-permute-done.from_left_ref = f32[8,64,128]{2,1,0:T(8,128)S(1)} collective-permute-done((f32[8,64,128]{2,1,0:T(8,128)}, f32[8,64,128]{2,1,0:T(8,128)S(1)}, u32[]{:S(2)}, u32[]{:S(2)}) %collective-permute-start) | collective-permute-done | bytes 262176 | tf_op jit(solution)/shard_map/ppermute | solution.py:332
  16.8 2.5 %join_kernel.1 = (f32[8,2,64,128]{3,2,1,0:T(8,128)}, f32[8,2,64,128]{3,2,1,0:T(8,128)}) custom-call(f32[4,128,128]{2,1,0:T(8,128)} %real_ref.5, f32[4,128,128]{2,1,0:T(8,128)} %imag_ref.5, f32[8,64,128]{2,1,0:T(8,128)} %copy-done.5, f32[8,64,128]{2,1,0:T(8,128)} %copy-done.6), custom_call_target="tpu_custom_call" | custom-call | flops 1000000 | bytes 1000000 | tf_op jit(solution)/shard_map/join_kernel/pallas_call | solution.py:316
  19.3 1.7 %collective-permute-start.3 = (f32[8,2,64,128]{3,2,1,0:T(8,128)}, f32[8,2,64,128]{3,2,1,0:T(8,128)S(1)}, u32[]{:S(2)}, u32[]{:S(2)}) collective-permute-start(f32[8,2,64,128]{3,2,1,0:T(8,128)} %get-tuple-element.20.top_ref), channel_id=1, source_target_pairs={{0,112},{16,0},{32,16},{48,32},{64,48},{80,64},{96,80},{112,96},{1... | collective-permute-start | bytes 1572872 | tf_op jit(solution)/shard_map/ppermute | solution.py:332
  22.9 5.2 %collective-permute-done.2.up_ref = f32[8,2,64,128]{3,2,1,0:T(8,128)S(1)} collective-permute-done((f32[8,2,64,128]{3,2,1,0:T(8,128)}, f32[8,2,64,128]{3,2,1,0:T(8,128)S(1)}, u32[]{:S(2)}, u32[]{:S(2)}) %collective-permute-start.2) | collective-permute-done | bytes 524320 | tf_op jit(solution)/shard_map/ppermute | solution.py:332
  29.7 17.6 %main_kernel.1 = (f32[8,2,72,128]{3,2,1,0:T(8,128)}, f32[8,2,72,128]{3,2,1,0:T(8,128)}, f32[8,2,128,128]{3,2,1,0:T(8,128)}, f32[128,128]{1,0:T(8,128)}, f32[128,128]{1,0:T(8,128)}) custom-call(s32[13]{0:T(128)} %concatenate.3.at_ref, f32[8,2,64,128]{3,2,1,0:T(8,128)} %copy-done.10, f32[8,2,64,128]{3,2,1,0:T(8,128)} %get-tuple-element.20.top_ref, ...), custom_call_target="tpu_custom_call" | custom-call | flops 12000000000 | bytes 1000000 | tf_op jit(solution)/shard_map/main_kernel/pallas_call | solution.py:316
  48.3 1.1 %collective-permute-done.8 = f32[128,128]{1,0:T(8,128)S(1)} collective-permute-done((f32[128,128]{1,0:T(8,128)}, f32[128,128]{1,0:T(8,128)S(1)}, u32[]{:S(2)}, u32[]{:S(2)}) %collective-permute-start.8) | collective-permute-done | bytes 65568 | tf_op jit(solution)/shard_map/ppermute | solution.py:355
  51.1 1.2 %collective-permute-start.10 = (f32[128,128]{1,0:T(8,128)S(1)}, f32[128,128]{1,0:T(8,128)S(1)}, u32[]{:S(2)}, u32[]{:S(2)}) collective-permute-start(f32[128,128]{1,0:T(8,128)S(1)} %add.37), channel_id=1, source_target_pairs={{0,4},{1,5},{2,6},{3,7},{4,8},{5,9},{6,10},{7,11},{8,12},{9,13},{1... | collective-permute-start | bytes 196616 | tf_op jit(solution)/shard_map/ppermute | solution.py:347
  53.1 1.7 %collective-permute-start.5 = (f32[8,2,72,128]{3,2,1,0:T(8,128)}, f32[8,2,72,128]{3,2,1,0:T(8,128)S(1)}, u32[]{:S(2)}, u32[]{:S(2)}) collective-permute-start(f32[8,2,72,128]{3,2,1,0:T(8,128)} %get-tuple-element.23), channel_id=1, source_target_pairs={{0,112},{16,0},{32,16},{48,32},{64,48},{80,64},{96,80},{112,96},{1... | collective-permute-start | bytes 1769480 | tf_op jit(solution)/shard_map/ppermute | solution.py:332
  54.8 2.4 %collective-permute-done.10 = f32[128,128]{1,0:T(8,128)S(1)} collective-permute-done((f32[128,128]{1,0:T(8,128)S(1)}, f32[128,128]{1,0:T(8,128)S(1)}, u32[]{:S(2)}, u32[]{:S(2)}) %collective-permute-start.10) | collective-permute-done | bytes 65568 | tf_op jit(solution)/shard_map/ppermute | solution.py:347
  58.1 3.9 %collective-permute-start.14 = (f32[128,128]{1,0:T(8,128)S(1)}, f32[128,128]{1,0:T(8,128)S(1)}, u32[]{:S(2)}, u32[]{:S(2)}) collective-permute-start(f32[128,128]{1,0:T(8,128)S(1)} %add_add_fusion.2), channel_id=1, source_target_pairs={{0,3},{1,0},{2,1},{3,2},{4,7},{5,4},{6,5},{7,6},{8,11},{9,8},{10,9... | collective-permute-start | bytes 196616 | tf_op jit(solution)/shard_map/ppermute | solution.py:347
  62.0 1.5 %collective-permute-start.12 = (f32[128,128]{1,0:T(8,128)S(1)}, f32[128,128]{1,0:T(8,128)S(1)}, u32[]{:S(2)}, u32[]{:S(2)}) collective-permute-start(f32[128,128]{1,0:T(8,128)S(1)} %add_add_fusion.2), channel_id=1, source_target_pairs={{0,2},{1,3},{2,0},{3,1},{4,6},{5,7},{6,4},{7,5},{8,10},{9,11},{10,... | collective-permute-start | bytes 196616 | tf_op jit(solution)/shard_map/ppermute | solution.py:347
  63.9 4.3 %collective-permute-done.13 = f32[128,128]{1,0:T(8,128)S(1)} collective-permute-done((f32[128,128]{1,0:T(8,128)S(1)}, f32[128,128]{1,0:T(8,128)S(1)}, u32[]{:S(2)}, u32[]{:S(2)}) %collective-permute-start.13) | collective-permute-done | bytes 65568 | tf_op jit(solution)/shard_map/ppermute | solution.py:347
  68.2 1.0 %collective-permute-start.17 = (f32[128,128]{1,0:T(8,128)S(1)}, f32[128,128]{1,0:T(8,128)S(1)}, u32[]{:S(2)}, u32[]{:S(2)}) collective-permute-start(f32[128,128]{1,0:T(8,128)S(1)} %add_add_fusion.1), channel_id=1, source_target_pairs={{0,96},{16,112},{32,0},{48,16},{64,32},{80,48},{96,64},{112,80},{1... | collective-permute-start | bytes 196616 | tf_op jit(solution)/shard_map/ppermute | solution.py:347
  69.1 1.1 %collective-permute-start.16 = (f32[128,128]{1,0:T(8,128)S(1)}, f32[128,128]{1,0:T(8,128)S(1)}, u32[]{:S(2)}, u32[]{:S(2)}) collective-permute-start(f32[128,128]{1,0:T(8,128)S(1)} %add_add_fusion.1), channel_id=1, source_target_pairs={{0,32},{16,48},{32,64},{48,80},{64,96},{80,112},{96,0},{112,16},{1... | collective-permute-start | bytes 196616 | tf_op jit(solution)/shard_map/ppermute | solution.py:347
  70.3 3.4 %collective-permute-start.15 = (f32[128,128]{1,0:T(8,128)S(1)}, f32[128,128]{1,0:T(8,128)S(1)}, u32[]{:S(2)}, u32[]{:S(2)}) collective-permute-start(f32[128,128]{1,0:T(8,128)S(1)} %add_add_fusion.1), channel_id=1, source_target_pairs={{0,64},{16,80},{32,96},{48,112},{64,0},{80,16},{96,32},{112,48},{1... | collective-permute-start | bytes 196616 | tf_op jit(solution)/shard_map/ppermute | solution.py:347
  74.6 3.3 %column_kernel.1 = (f32[8,72,128]{2,1,0:T(8,128)}, f32[8,72,128]{2,1,0:T(8,128)}, f32[8,128,128]{2,1,0:T(8,128)}) custom-call(s32[13]{0:T(128)} %concatenate.3.at_ref, f32[8,2,128,128]{3,2,1,0:T(8,128)} %get-tuple-element.21.mid_ref, f32[8,2,72,128]{3,2,1,0:T(8,128)} %copy-done, f32[8,2,72,128]{3,2,1,0:T(8,128)} %copy-done.1), custom_call_target="tpu_custom_call" | custom-call | flops 1000000 | bytes 1000000 | tf_op jit(solution)/shard_map/column_kernel/pallas_call | solution.py:316
  78.1 5.2 %collective-permute-start.7 = (f32[8,72,128]{2,1,0:T(8,128)}, f32[8,72,128]{2,1,0:T(8,128)S(1)}, u32[]{:S(2)}, u32[]{:S(2)}) collective-permute-start(f32[8,72,128]{2,1,0:T(8,128)} %get-tuple-element.26), channel_id=1, source_target_pairs={{0,15},{1,0},{2,1},{3,2},{4,3},{5,4},{6,5},{7,6},{8,7},{9,8},{10,9... | collective-permute-start | bytes 884744 | tf_op jit(solution)/shard_map/ppermute | solution.py:332
  83.5 1.2 %collective-permute-done.18.other_ref = f32[128,128]{1,0:T(8,128)S(1)} collective-permute-done((f32[128,128]{1,0:T(8,128)S(1)}, f32[128,128]{1,0:T(8,128)S(1)}, u32[]{:S(2)}, u32[]{:S(2)}) %collective-permute-start.18) | collective-permute-done | bytes 65568 | tf_op jit(solution)/shard_map/ppermute | solution.py:355
  85.3 1.8 %probe_kernel.1 = f32[2,128,128]{2,1,0:T(8,128)} custom-call(s32[13]{0:T(128)} %concatenate.3.at_ref, f32[128,128]{1,0:T(8,128)} %copy-done.4, f32[128,128]{1,0:T(8,128)} %copy-done.8, f32[2,128,128]{2,1,0:T(8,128)} %probe_ref.3), custom_call_target="tpu_custom_call" | custom-call | flops 1000000 | bytes 1000000 | tf_op jit(solution)/shard_map/probe_kernel/pallas_call | solution.py:316
  87.1 1.1 %collective-permute-done.6.from_left_ref = f32[8,72,128]{2,1,0:T(8,128)S(1)} collective-permute-done((f32[8,72,128]{2,1,0:T(8,128)}, f32[8,72,128]{2,1,0:T(8,128)S(1)}, u32[]{:S(2)}, u32[]{:S(2)}) %collective-permute-start.6) | collective-permute-done | bytes 294944 | tf_op jit(solution)/shard_map/ppermute | solution.py:332
  89.0 2.3 %final_kernel.1 = (f32[4,128,128]{2,1,0:T(8,128)}, f32[4,128,128]{2,1,0:T(8,128)}) custom-call(f32[4,128,128]{2,1,0:T(8,128)} %real_ref.5, f32[4,128,128]{2,1,0:T(8,128)} %imag_ref.5, f32[8,128,128]{2,1,0:T(8,128)} %get-tuple-element.24.center_ref, f32[8,72,128]{2,1,0:T(8,128)} %copy-done.2, f32[8,72,128]{2,1,0:T(8,128)} %copy-done.3), custom_call_target="tpu_custom_call" | custom-call | flops 1000000 | bytes 1000000 | tf_op jit(solution)/shard_map/final_kernel/pallas_call | solution.py:316
  (55 shorter events, 12.3 us)
Async XLA Ops:
  2.6 12.7 %collective-permute-start = (f32[8,64,128]{2,1,0:T(8,128)}, f32[8,64,128]{2,1,0:T(8,128)S(1)}, u32[]{:S(2)}, u32[]{:S(2)}) collective-permute-start(f32[8,64,128]{2,1,0:T(8,128)} %get-tuple-element.17), channel_id=1, source_target_pairs={{0,1},{1,2},{2,3},{3,4},{4,5},{5,6},{6,7},{7,8},{8,9},{9,10},{10,1... | collective-permute-start | bytes 786440 | tf_op jit(solution)/shard_map/ppermute | solution.py:332
  4.6 10.8 %collective-permute-start.1 = (f32[8,64,128]{2,1,0:T(8,128)}, f32[8,64,128]{2,1,0:T(8,128)S(1)}, u32[]{:S(2)}, u32[]{:S(2)}) collective-permute-start(f32[8,64,128]{2,1,0:T(8,128)} %get-tuple-element.18), channel_id=1, source_target_pairs={{0,15},{1,0},{2,1},{3,2},{4,3},{5,4},{6,5},{7,6},{8,7},{9,8},{10,9... | collective-permute-start | bytes 786440 | tf_op jit(solution)/shard_map/ppermute | solution.py:332
  16.8 5.2 %copy-start.7 = (f32[128,128]{1,0:T(8,128)S(1)}, f32[128,128]{1,0:T(8,128)}, u32[]{:S(2)}) copy-start(f32[128,128]{1,0:T(8,128)} %param.10) | copy-start | bytes 196612
  19.3 1.8 %copy-start.9 = (s32[4,2]{0,1:T(2,128)S(1)}, s32[4,2]{0,1:T(2,128)}, u32[]{:S(2)}) copy-start(s32[4,2]{0,1:T(2,128)} %param.8) | copy-start | bytes 100
  19.3 8.8 %collective-permute-start.2 = (f32[8,2,64,128]{3,2,1,0:T(8,128)}, f32[8,2,64,128]{3,2,1,0:T(8,128)S(1)}, u32[]{:S(2)}, u32[]{:S(2)}) collective-permute-start(f32[8,2,64,128]{3,2,1,0:T(8,128)} %get-tuple-element.19.bottom_ref), channel_id=1, source_target_pairs={{0,16},{16,32},{32,48},{48,64},{64,80},{80,96},{96,112},{112,0},{1... | collective-permute-start | bytes 1572872 | tf_op jit(solution)/shard_map/ppermute | solution.py:332
  19.3 8.8 %collective-permute-start.3 = (f32[8,2,64,128]{3,2,1,0:T(8,128)}, f32[8,2,64,128]{3,2,1,0:T(8,128)S(1)}, u32[]{:S(2)}, u32[]{:S(2)}) collective-permute-start(f32[8,2,64,128]{3,2,1,0:T(8,128)} %get-tuple-element.20.top_ref), channel_id=1, source_target_pairs={{0,112},{16,0},{32,16},{48,32},{64,48},{80,64},{96,80},{112,96},{1... | collective-permute-start | bytes 1572872 | tf_op jit(solution)/shard_map/ppermute | solution.py:332
  47.3 2.1 %collective-permute-start.8 = (f32[128,128]{1,0:T(8,128)}, f32[128,128]{1,0:T(8,128)S(1)}, u32[]{:S(2)}, u32[]{:S(2)}) collective-permute-start(f32[128,128]{1,0:T(8,128)} %get-tuple-element.30), channel_id=1, source_target_pairs={{0,16},{16,0},{32,48},{48,32},{64,80},{80,64},{96,112},{112,96},{1... | collective-permute-start | bytes 196616 | tf_op jit(solution)/shard_map/ppermute | solution.py:355
  50.2 4.6 %collective-permute-start.11 = (f32[128,128]{1,0:T(8,128)S(1)}, f32[128,128]{1,0:T(8,128)S(1)}, u32[]{:S(2)}, u32[]{:S(2)}) collective-permute-start(f32[128,128]{1,0:T(8,128)S(1)} %add.37), channel_id=1, source_target_pairs={{0,12},{1,13},{2,14},{3,15},{4,0},{5,1},{6,2},{7,3},{8,4},{9,5},{1... | collective-permute-start | bytes 196616 | tf_op jit(solution)/shard_map/ppermute | solution.py:347
  51.1 6.2 %collective-permute-start.10 = (f32[128,128]{1,0:T(8,128)S(1)}, f32[128,128]{1,0:T(8,128)S(1)}, u32[]{:S(2)}, u32[]{:S(2)}) collective-permute-start(f32[128,128]{1,0:T(8,128)S(1)} %add.37), channel_id=1, source_target_pairs={{0,4},{1,5},{2,6},{3,7},{4,8},{5,9},{6,10},{7,11},{8,12},{9,13},{1... | collective-permute-start | bytes 196616 | tf_op jit(solution)/shard_map/ppermute | solution.py:347
  52.3 5.8 %collective-permute-start.9 = (f32[128,128]{1,0:T(8,128)S(1)}, f32[128,128]{1,0:T(8,128)S(1)}, u32[]{:S(2)}, u32[]{:S(2)}) collective-permute-start(f32[128,128]{1,0:T(8,128)S(1)} %add.37), channel_id=1, source_target_pairs={{0,8},{1,9},{2,10},{3,11},{4,12},{5,13},{6,14},{7,15},{8,0},{9,1},... | collective-permute-start | bytes 196616 | tf_op jit(solution)/shard_map/ppermute | solution.py:347
  53.1 20.5 %collective-permute-start.4 = (f32[8,2,72,128]{3,2,1,0:T(8,128)}, f32[8,2,72,128]{3,2,1,0:T(8,128)S(1)}, u32[]{:S(2)}, u32[]{:S(2)}) collective-permute-start(f32[8,2,72,128]{3,2,1,0:T(8,128)} %get-tuple-element.22), channel_id=1, source_target_pairs={{0,16},{16,32},{32,48},{48,64},{64,80},{80,96},{96,112},{112,0},{1... | collective-permute-start | bytes 1769480 | tf_op jit(solution)/shard_map/ppermute | solution.py:332
  53.1 20.5 %collective-permute-start.5 = (f32[8,2,72,128]{3,2,1,0:T(8,128)}, f32[8,2,72,128]{3,2,1,0:T(8,128)S(1)}, u32[]{:S(2)}, u32[]{:S(2)}) collective-permute-start(f32[8,2,72,128]{3,2,1,0:T(8,128)} %get-tuple-element.23), channel_id=1, source_target_pairs={{0,112},{16,0},{32,16},{48,32},{64,48},{80,64},{96,80},{112,96},{1... | collective-permute-start | bytes 1769480 | tf_op jit(solution)/shard_map/ppermute | solution.py:332
  58.1 5.8 %collective-permute-start.14 = (f32[128,128]{1,0:T(8,128)S(1)}, f32[128,128]{1,0:T(8,128)S(1)}, u32[]{:S(2)}, u32[]{:S(2)}) collective-permute-start(f32[128,128]{1,0:T(8,128)S(1)} %add_add_fusion.2), channel_id=1, source_target_pairs={{0,3},{1,0},{2,1},{3,2},{4,7},{5,4},{6,5},{7,6},{8,11},{9,8},{10,9... | collective-permute-start | bytes 196616 | tf_op jit(solution)/shard_map/ppermute | solution.py:347
  62.0 6.2 %collective-permute-start.13 = (f32[128,128]{1,0:T(8,128)S(1)}, f32[128,128]{1,0:T(8,128)S(1)}, u32[]{:S(2)}, u32[]{:S(2)}) collective-permute-start(f32[128,128]{1,0:T(8,128)S(1)} %add_add_fusion.2), channel_id=1, source_target_pairs={{0,1},{1,2},{2,3},{3,0},{4,5},{5,6},{6,7},{7,4},{8,9},{9,10},{10,1... | collective-permute-start | bytes 196616 | tf_op jit(solution)/shard_map/ppermute | solution.py:347
  62.0 6.2 %collective-permute-start.12 = (f32[128,128]{1,0:T(8,128)S(1)}, f32[128,128]{1,0:T(8,128)S(1)}, u32[]{:S(2)}, u32[]{:S(2)}) collective-permute-start(f32[128,128]{1,0:T(8,128)S(1)} %add_add_fusion.2), channel_id=1, source_target_pairs={{0,2},{1,3},{2,0},{3,1},{4,6},{5,7},{6,4},{7,5},{8,10},{9,11},{10,... | collective-permute-start | bytes 196616 | tf_op jit(solution)/shard_map/ppermute | solution.py:347
  68.2 15.1 %collective-permute-start.17 = (f32[128,128]{1,0:T(8,128)S(1)}, f32[128,128]{1,0:T(8,128)S(1)}, u32[]{:S(2)}, u32[]{:S(2)}) collective-permute-start(f32[128,128]{1,0:T(8,128)S(1)} %add_add_fusion.1), channel_id=1, source_target_pairs={{0,96},{16,112},{32,0},{48,16},{64,32},{80,48},{96,64},{112,80},{1... | collective-permute-start | bytes 196616 | tf_op jit(solution)/shard_map/ppermute | solution.py:347
  69.1 14.2 %collective-permute-start.16 = (f32[128,128]{1,0:T(8,128)S(1)}, f32[128,128]{1,0:T(8,128)S(1)}, u32[]{:S(2)}, u32[]{:S(2)}) collective-permute-start(f32[128,128]{1,0:T(8,128)S(1)} %add_add_fusion.1), channel_id=1, source_target_pairs={{0,32},{16,48},{32,64},{48,80},{64,96},{80,112},{96,0},{112,16},{1... | collective-permute-start | bytes 196616 | tf_op jit(solution)/shard_map/ppermute | solution.py:347
  70.3 13.1 %collective-permute-start.15 = (f32[128,128]{1,0:T(8,128)S(1)}, f32[128,128]{1,0:T(8,128)S(1)}, u32[]{:S(2)}, u32[]{:S(2)}) collective-permute-start(f32[128,128]{1,0:T(8,128)S(1)} %add_add_fusion.1), channel_id=1, source_target_pairs={{0,64},{16,80},{32,96},{48,112},{64,0},{80,16},{96,32},{112,48},{1... | collective-permute-start | bytes 196616 | tf_op jit(solution)/shard_map/ppermute | solution.py:347
  73.6 0.8 copy-start
  73.6 1.0 %copy-start.1 = (f32[8,2,72,128]{3,2,1,0:T(8,128)}, f32[8,2,72,128]{3,2,1,0:T(8,128)S(1)}, u32[]{:S(2)}) copy-start(f32[8,2,72,128]{3,2,1,0:T(8,128)S(1)} %collective-permute-done.5.from_down_ref) | copy-start | bytes 1769476
  78.0 10.3 %collective-permute-start.6 = (f32[8,72,128]{2,1,0:T(8,128)}, f32[8,72,128]{2,1,0:T(8,128)S(1)}, u32[]{:S(2)}, u32[]{:S(2)}) collective-permute-start(f32[8,72,128]{2,1,0:T(8,128)} %get-tuple-element.25), channel_id=1, source_target_pairs={{0,1},{1,2},{2,3},{3,4},{4,5},{5,6},{6,7},{7,8},{8,9},{9,10},{10,1... | collective-permute-start | bytes 884744 | tf_op jit(solution)/shard_map/ppermute | solution.py:332
  78.1 10.1 %collective-permute-start.7 = (f32[8,72,128]{2,1,0:T(8,128)}, f32[8,72,128]{2,1,0:T(8,128)S(1)}, u32[]{:S(2)}, u32[]{:S(2)}) collective-permute-start(f32[8,72,128]{2,1,0:T(8,128)} %get-tuple-element.26), channel_id=1, source_target_pairs={{0,15},{1,0},{2,1},{3,2},{4,3},{5,4},{6,5},{7,6},{8,7},{9,8},{10,9... | collective-permute-start | bytes 884744 | tf_op jit(solution)/shard_map/ppermute | solution.py:332
  83.3 1.3 %copy-start.4 = (f32[128,128]{1,0:T(8,128)}, f32[128,128]{1,0:T(8,128)S(1)}, u32[]{:S(2)}) copy-start(f32[128,128]{1,0:T(8,128)S(1)} %add_add_fusion.own_ref) | copy-start | bytes 196612
  83.4 1.3 %collective-permute-start.18 = (f32[128,128]{1,0:T(8,128)S(1)}, f32[128,128]{1,0:T(8,128)S(1)}, u32[]{:S(2)}, u32[]{:S(2)}) collective-permute-start(f32[128,128]{1,0:T(8,128)S(1)} %add_add_fusion.own_ref), channel_id=1, source_target_pairs={{0,16},{16,0},{32,48},{48,32},{64,80},{80,64},{96,112},{112,96},{1... | collective-permute-start | bytes 196616 | tf_op jit(solution)/shard_map/ppermute | solution.py:355
  (7 other events, 5.2 us)
